TPU v7x, 32 devices: a whole 2x2x4 slice. The times are simulated.
32 devices in a mesh: prompt: 4 (over z), sample: 4 (over x, core), vocab: 2 (over y).
Axes of the slice: x: 2, y: 2, z: 4, core: 2. Of those that a mesh axis runs over, the one named last changes fastest.
Arguments:
- hidden: bfloat16 [4, 24, 3584], P('sample', ('prompt', 'vocab')), may hold values from -170 to 170
- unembed: bfloat16 [152064, 3584], P(('prompt', 'vocab')), may hold values from -1 to 1
- token_ids: int32 [4, 24], P('sample', ('prompt', 'vocab')), may hold values from 0 to 152063, as said below
- old_logp: float32 [4, 24], P('sample', ('prompt', 'vocab')), may hold values from -14 to -11
- ref_logp: float32 [4, 24], P('sample', ('prompt', 'vocab')), may hold values from -14 to -11
- loss_mask: int32 [4, 24], P('sample', ('prompt', 'vocab')), may hold values 0 or 1
- lengths: int32 [4, 4], P('prompt', 'sample'), may hold values from 1 to 6, as said below
- sample_valid: int32 [4, 4], P('prompt', 'sample'), may hold values 0 or 1
- rewards: int32 [4, 4], P('prompt', 'sample'), may hold values from -300 to 300
Outputs:
- token_logp: float32 [4, 24], P('sample', ('prompt', 'vocab'))
- token_loss: float32 [4, 24], P('sample', ('prompt', 'vocab'))
- advantages: float32 [4, 4], P('prompt', 'sample')
- loss: float32 [], replicated
Inputs may be any that keep to these rules, and one draw needn't show every extreme that they name: `token_ids`: token ids name vocabulary entries. `lengths`: some response in every draw has length 6.
All inputs are finite; a program needn't handle non-finite values. No bound on the sum of `loss_mask` or of `sample_valid` on one device may be relied on, other than what follows from the above.
Results may differ from a plain program's by a relative error of at most 0.0003.
Values may be sent and summed in bfloat16 or wider, within the bound.
A program may use at most 192 MiB of HBM per device.

v0:
```python
import jax
import jax.numpy as jnp
from jax import lax
from jax.sharding import PartitionSpec as P

clip_low = 0.8
clip_high = 1.2
dual_clip = 3.0
kl_weight = 0.04
reward_unit = 0.01
std_floor = 0.5


def combined_all(value, axis, join):
    pieces = jax.tree.map(lambda part: lax.all_gather(part, axis), value)
    head = jax.tree.map(lambda part: part[0], pieces)
    tail = jax.tree.map(lambda part: part[1:], pieces)
    total, _ = lax.scan(lambda total, slab: (join(total, slab), None), head, tail)
    return total


def shard_stats(row_block, labels, weight, vocab_start):
    logits = lax.dot_general(
        row_block, weight, (((1,), (1,)), ((), ())), preferred_element_type=jnp.float32
    )
    local_peak = jnp.max(logits, axis=1)
    exp_total = jnp.sum(jnp.exp(logits - local_peak[:, None]), axis=1)
    column = vocab_start + lax.broadcasted_iota(jnp.int32, logits.shape, 1)
    target = jnp.sum(jnp.where(column == labels[:, None], logits, 0.0), axis=1)
    return (local_peak, exp_total, target)


def merge_pairs(first_part, second_part):
    peak_one, total_one, target_one = first_part
    peak_two, total_two, target_two = second_part
    joined_peak = jnp.maximum(peak_one, peak_two)
    joined_total = total_one * jnp.exp(peak_one - joined_peak) + total_two * jnp.exp(
        peak_two - joined_peak
    )
    return (joined_peak, joined_total, target_one + target_two)


def local(
    hidden, unembed, token_ids, old_logp, ref_logp, loss_mask, lengths, sample_valid, rewards
):
    samples, local_rows, width = hidden.shape
    vocab_rows = unembed.shape[0]
    vocab_start = lax.axis_index(("prompt", "vocab")) * vocab_rows
    positions = lax.axis_index("vocab") * local_rows + lax.broadcasted_iota(
        jnp.int32, (samples, local_rows), 1
    )
    live_rows = (loss_mask == 1) & (positions < lengths.T) & (sample_valid.T == 1)
    live_float = live_rows.astype(jnp.float32)
    valid_f = sample_valid.astype(jnp.float32)
    scores = rewards.astype(jnp.float32) * reward_unit
    group_count, first_moment, second_moment = lax.psum(
        (
            jnp.sum(valid_f, axis=1),
            jnp.sum(valid_f * scores, axis=1),
            jnp.sum(valid_f * scores * scores, axis=1),
        ),
        "sample",
    )
    safe_count = jnp.maximum(group_count, 1.0)
    group_mean = first_moment / safe_count
    spread = jnp.sqrt(jnp.maximum(second_moment / safe_count - group_mean * group_mean, 0.0))
    advantages = valid_f * (scores - group_mean[:, None]) / jnp.maximum(spread, std_floor)[:, None]
    part_hidden = lax.all_gather(hidden, ("prompt", "vocab"), axis=1, tiled=True)
    part_ids = lax.all_gather(token_ids, ("prompt", "vocab"), axis=1, tiled=True)
    piece_rows = part_hidden.shape[1]
    piece_stats = shard_stats(
        part_hidden.reshape(samples * piece_rows, width),
        part_ids.reshape(samples * piece_rows),
        unembed,
        vocab_start,
    )
    peak_new = piece_stats[0].reshape(samples, piece_rows)
    total_new = piece_stats[1].reshape(samples, piece_rows)
    target_new = piece_stats[2].reshape(samples, piece_rows)
    row_top, total_all, target_all = combined_all(
        (peak_new, total_new, target_new), ("prompt", "vocab"), merge_pairs
    )
    own_start = lax.axis_index(("prompt", "vocab")) * local_rows

    def own_rows(values):
        return lax.dynamic_slice_in_dim(values, own_start, local_rows, 1)

    raw_logp = own_rows(target_all) - (own_rows(row_top) + jnp.log(own_rows(total_all)))
    token_logp = jnp.where(live_rows, raw_logp, 0.0)
    adv_rows = advantages.T
    prob_ratio = jnp.exp(raw_logp - old_logp)
    gain_side = adv_rows * jnp.minimum(prob_ratio, clip_high)
    loss_side = jnp.maximum(adv_rows * jnp.maximum(prob_ratio, clip_low), dual_clip * adv_rows)
    objective = jnp.where(adv_rows >= 0.0, gain_side, loss_side)
    log_gap = ref_logp - raw_logp
    kl_term = jnp.exp(log_gap) - log_gap - 1.0
    token_loss = jnp.where(live_rows, kl_weight * kl_term - objective, 0.0)
    loss_part = jnp.sum(token_loss)
    loss_total, live_total = lax.psum(
        (loss_part, jnp.sum(live_float)), ("prompt", "sample", "vocab")
    )
    loss = loss_total / jnp.maximum(live_total, 1.0)
    return (token_logp, token_loss, advantages, loss)


def solution(mesh):
    in_specs = (
        P("sample", ("prompt", "vocab"), None),
        P(("prompt", "vocab"), None),
        P("sample", ("prompt", "vocab")),
        P("sample", ("prompt", "vocab")),
        P("sample", ("prompt", "vocab")),
        P("sample", ("prompt", "vocab")),
        P("prompt", "sample"),
        P("prompt", "sample"),
        P("prompt", "sample"),
    )
    out_specs = (
        P("sample", ("prompt", "vocab")),
        P("sample", ("prompt", "vocab")),
        P("prompt", "sample"),
        P(),
    )
    return jax.shard_map(local, mesh=mesh, in_specs=in_specs, out_specs=out_specs, check_vma=False)
```

profile of v0, /device:TPU:12, one launch (start us, length us, event | category | flops | bytes accessed | tf_op | source)
XLA Modules:
  0.0 173.8 jit_solution(1254609279268593562)
XLA Ops:
  1.9 1.3 convert_reduce_fusion
  3.9 9.1 %all-reduce.6 = (f32[1]{0:T(128)}, f32[1]{0:T(128)}, f32[1]{0:T(128)}) all-reduce(f32[1]{0:T(128)} %bitcast.11, f32[1]{0:T(128)} %bitcast.12, f32[1]{0:T(128)} %bitcast.14), channel_id=1, replica_groups=mesh['prompt'=4,'sample'=4,'vocab'=2] {'sample'}, use_global_device_ids=true, to_apply=%region_5.0 | all-reduce | flops 3 | bytes 24 | tf_op jit(solution)/shard_map/psum | solution.py:56
  15.0 0.8 copy.14
  15.8 28.5 %all_gather.15 = bf16[1,24,3584]{2,0,1:T(2,128)(2,1)S(1)} all-gather(bf16[1,3,3584]{2,0,1:T(2,128)(2,1)S(1)} %copy.14), channel_id=1, replica_groups=mesh['prompt'=4,'sample'=4,'vocab'=2] {'prompt','vocab'}, dimensions={1}, use_global_device_ids=true | all-gather | bytes 193536 | tf_op jit(solution)/shard_map/all_gather | solution.py:68
  44.3 0.0 copy-start.3
  44.3 0.0 copy-start.2
  44.3 48.0 %fusion.21 = (f32[24]{0:T(128)S(1)}, f32[24,19008]{1,0:T(8,128)S(1)}) fusion(bf16[19008,3584]{1,0:T(8,128)(2,1)} %param.12, bf16[1,24,3584]{2,0,1:T(2,128)(2,1)S(1)} %all_gather.15), kind=kOutput, calls=%fused_computation.36 | convolution fusion | flops 3270440448 | bytes 138246240 | tf_op jit(solution)/shard_map/dot_general | solution.py:23
  92.3 0.0 copy-start
  92.3 0.0 copy-start.1
  92.3 0.0 copy-done.3
  92.3 0.6 dynamic-slice
  93.6 0.2 dynamic-update-slice
  94.5 0.0 copy-done.2
  94.5 0.1 bitcast_dynamic-update-slice_fusion
  94.6 11.2 %all-reduce.2 = s32[24]{0:T(128)S(1)} all-reduce(s32[24]{0:T(128)S(1)} %bitcast_dynamic-update-slice_fusion), channel_id=1, replica_groups=mesh['prompt'=4,'sample'=4,'vocab'=2] {'prompt','vocab'}, use_global_device_ids=true, to_apply=%add.2 | all-reduce | flops 24 | bytes 192
  105.8 0.7 select_reduce_fusion
  106.6 0.2 dynamic-update-slice.1
  106.8 0.2 dynamic-update-slice.3
  107.0 17.1 %all-reduce.5 = (f32[192]{0:T(256)S(1)}, f32[192]{0:T(256)S(1)}, f32[192]{0:T(256)S(1)}) all-reduce(f32[192]{0:T(256)S(1)} %dynamic-update-slice, f32[192]{0:T(256)S(1)} %dynamic-update-slice.1, f32[192]{0:T(256)S(1)} %dynamic-update-slice.3), channel_id=2, replica_groups=mesh['prompt'=4,'sample'=4,'vocab'=2] {'prompt','vocab'}, use_global_device_ids=true, to_apply=%add | all-reduce | flops 576 | bytes 4608
  124.1 0.1 slice.27
  124.2 0.1 reshape.48
  124.3 0.1 slice.28
  124.4 0.1 reshape.49
  124.5 0.1 slice.29
  124.5 0.1 reshape.50
  124.6 0.3 while.14
  124.9 0.0 copy-done
  124.9 0.0 copy-done.1
  124.9 1.2 fusion.18
  126.1 0.5 broadcast_select_fusion.1
  126.6 43.7 %all-reduce.4 = (f32[]{:T(128)}, f32[]{:T(128)}) all-reduce(f32[]{:T(128)} %get-tuple-element.74, f32[]{:T(128)} %get-tuple-element.72), channel_id=1, replica_groups=mesh['prompt'=4,'sample'=4,'vocab'=2] {'prompt','sample','vocab'}, use_global_device_ids=true, to_apply=%region_9.10 | all-reduce | flops 2 | bytes 16 | tf_op jit(solution)/shard_map/psum | solution.py:99
  (14 shorter events, 0.2 us)
Async XLA Ops:
  44.3 48.0 %copy-start.3 = (u32[32]{0:T(128)S(1)}, u32[32]{0:T(128)}, u32[]{:S(2)}) copy-start(u32[32]{0:T(128)} %constant.69) | copy-start | bytes 388
  44.3 50.2 %copy-start.2 = (s32[1,3]{1,0:T(1,128)S(1)}, s32[1,3]{1,0:T(1,128)}, u32[]{:S(2)}) copy-start(s32[1,3]{1,0:T(1,128)} %param.13) | copy-start | bytes 40
  92.3 32.6 %copy-start = (f32[1,3]{1,0:T(1,128)S(1)}, f32[1,3]{1,0:T(1,128)}, u32[]{:S(2)}) copy-start(f32[1,3]{1,0:T(1,128)} %param.14) | copy-start | bytes 40
  92.3 32.6 %copy-start.1 = (f32[1,3]{1,0:T(1,128)S(1)}, f32[1,3]{1,0:T(1,128)}, u32[]{:S(2)}) copy-start(f32[1,3]{1,0:T(1,128)} %param.15) | copy-start | bytes 40
where the time goes:
time: 174 us
  blocking collectives  110 us (63%)
  matrix products  48 us (28%)
  between operations  9.57 us (6%)
  other arithmetic  3.97 us (2%)
  local copies, waits for them, and re-layouts  2.71 us (2%)
    dot_general x1, matrix products, shard_stats(): lax.dot_general(row_block, weight, (((1,), (1,)), ((), ())), preferred_el...  48 us
    psum x1, blocking collectives, local(): lax.psum((loss_part, jnp.sum(live_float)), ('prompt', 'sample', 'vocab'))  43.7 us
    all_gather x1, blocking collectives, local(): lax.all_gather(hidden, ('prompt', 'vocab'), axis=1, tiled=True)  28.5 us
    unnamed x2, blocking collectives  28.4 us
    psum x1, blocking collectives, local(): lax.psum((jnp.sum(valid_f, axis=1), jnp.sum(valid_f * scores, axis=1), jn...  9.06 us

commit v1 on v0

--- a/solution.py
+++ b/solution.py
@@ -9,6 +9,12 @@
 kl_weight = 0.04
 reward_unit = 0.01
 std_floor = 0.5
+
+
+def post_goods_all(u):
+    next_value = lax.psum(u, "prompt")
+    piece_out = lax.psum(next_value, ("sample", "vocab"))
+    return piece_out
 
 
 def combined_all(value, axis, join):
@@ -96,9 +102,7 @@
     kl_term = jnp.exp(log_gap) - log_gap - 1.0
     token_loss = jnp.where(live_rows, kl_weight * kl_term - objective, 0.0)
     loss_part = jnp.sum(token_loss)
-    loss_total, live_total = lax.psum(
-        (loss_part, jnp.sum(live_float)), ("prompt", "sample", "vocab")
-    )
+    loss_total, live_total = post_goods_all((loss_part, jnp.sum(live_float)))
     loss = loss_total / jnp.maximum(live_total, 1.0)
     return (token_logp, token_loss, advantages, loss)
 

time: 174 us -> 159 us (0.914)
  blocking collectives: 110 us -> 92.9 us
    psum x1 -> x2, blocking collectives: 43.7 us -> 27 us  [the longest x1 14.9 us: post_goods_all(): piece_out = lax.psum(next_value, ('sample', 'vocab'))]
where the time goes in v1:
time: 159 us; the launch traced here: 157 us
  blocking collectives  92.9 us (58%)
  matrix products  48 us (30%)
  between operations  9.62 us (6%)
  other arithmetic  4 us (3%)
  local copies, waits for them, and re-layouts  2.71 us (2%)
    dot_general x1, matrix products, shard_stats(): lax.dot_general(row_block, weight, (((1,), (1,)), ((), ())), preferred_el...  48 us
    all_gather x1, blocking collectives, local(): lax.all_gather(hidden, ('prompt', 'vocab'), axis=1, tiled=True)  28.5 us
    unnamed x2, blocking collectives  28.4 us
    psum x1, blocking collectives, post_goods_all(): piece_out = lax.psum(next_value, ('sample', 'vocab'))  14.9 us
    psum x1, blocking collectives, post_goods_all(): next_value = lax.psum(u, 'prompt')  12.2 us
    psum x1, blocking collectives, local(): lax.psum((jnp.sum(valid_f, axis=1), jnp.sum(valid_f * scores, axis=1), jn...  9.01 us

profile of v1, /device:TPU:12, one launch (start us, length us, event | category | flops | bytes accessed | tf_op | source)
XLA Modules:
  0.0 157.3 jit_solution(12646879372017633839)
XLA Ops:
  1.9 1.3 convert_reduce_fusion
  3.9 9.0 %all-reduce.6 = (f32[1]{0:T(128)}, f32[1]{0:T(128)}, f32[1]{0:T(128)}) all-reduce(f32[1]{0:T(128)} %bitcast.11, f32[1]{0:T(128)} %bitcast.12, f32[1]{0:T(128)} %bitcast.14), channel_id=1, replica_groups=mesh['prompt'=4,'sample'=4,'vocab'=2] {'sample'}, use_global_device_ids=true, to_apply=%region_5.0 | all-reduce | flops 3 | bytes 24 | tf_op jit(solution)/shard_map/psum | solution.py:62
  15.0 0.8 copy.14
  15.8 28.5 %all_gather.15 = bf16[1,24,3584]{2,0,1:T(2,128)(2,1)S(1)} all-gather(bf16[1,3,3584]{2,0,1:T(2,128)(2,1)S(1)} %copy.14), channel_id=1, replica_groups=mesh['prompt'=4,'sample'=4,'vocab'=2] {'prompt','vocab'}, dimensions={1}, use_global_device_ids=true | all-gather | bytes 193536 | tf_op jit(solution)/shard_map/all_gather | solution.py:74
  44.3 0.0 copy-start.3
  44.3 0.0 copy-start.2
  44.3 48.0 %fusion.21 = (f32[24]{0:T(128)S(1)}, f32[24,19008]{1,0:T(8,128)S(1)}) fusion(bf16[19008,3584]{1,0:T(8,128)(2,1)} %param.12, bf16[1,24,3584]{2,0,1:T(2,128)(2,1)S(1)} %all_gather.15), kind=kOutput, calls=%fused_computation.36 | convolution fusion | flops 3270440448 | bytes 138246240 | tf_op jit(solution)/shard_map/dot_general | solution.py:29
  92.2 0.0 copy-start
  92.2 0.0 copy-start.1
  92.3 0.0 copy-done.3
  92.3 0.6 dynamic-slice
  93.5 0.2 dynamic-update-slice
  94.4 0.0 copy-done.2
  94.4 0.1 bitcast_dynamic-update-slice_fusion
  94.5 11.2 %all-reduce.2 = s32[24]{0:T(128)S(1)} all-reduce(s32[24]{0:T(128)S(1)} %bitcast_dynamic-update-slice_fusion), channel_id=1, replica_groups=mesh['prompt'=4,'sample'=4,'vocab'=2] {'prompt','vocab'}, use_global_device_ids=true, to_apply=%add.2 | all-reduce | flops 24 | bytes 192
  105.8 0.7 select_reduce_fusion
  106.5 0.2 dynamic-update-slice.1
  106.8 0.2 dynamic-update-slice.3
  107.0 17.1 %all-reduce.5 = (f32[192]{0:T(256)S(1)}, f32[192]{0:T(256)S(1)}, f32[192]{0:T(256)S(1)}) all-reduce(f32[192]{0:T(256)S(1)} %dynamic-update-slice, f32[192]{0:T(256)S(1)} %dynamic-update-slice.1, f32[192]{0:T(256)S(1)} %dynamic-update-slice.3), channel_id=2, replica_groups=mesh['prompt'=4,'sample'=4,'vocab'=2] {'prompt','vocab'}, use_global_device_ids=true, to_apply=%add | all-reduce | flops 576 | bytes 4608
  124.1 0.1 slice.27
  124.2 0.1 reshape.48
  124.2 0.1 slice.28
  124.3 0.1 reshape.49
  124.4 0.1 slice.29
  124.5 0.1 reshape.50
  124.6 0.3 while.14
  124.8 0.0 copy-done
  124.9 0.0 copy-done.1
  124.9 1.2 fusion.18
  126.1 0.5 broadcast_select_fusion.1
  126.6 12.2 %all-reduce.7 = (f32[]{:T(128)}, f32[]{:T(128)}) all-reduce(f32[]{:T(128)} %get-tuple-element.76, f32[]{:T(128)} %get-tuple-element.74), channel_id=1, replica_groups=mesh['prompt'=4,'sample'=4,'vocab'=2] {'prompt'}, use_global_device_ids=true, to_apply=%region_9.10 | all-reduce | flops 2 | bytes 16 | tf_op jit(solution)/shard_map/psum | solution.py:15
  138.8 14.9 %all-reduce.4 = (f32[]{:T(128)}, f32[]{:T(128)}) all-reduce(f32[]{:T(128)} %get-tuple-element.70, f32[]{:T(128)} %get-tuple-element.71), channel_id=1, replica_groups=mesh['prompt'=4,'sample'=4,'vocab'=2] {'sample','vocab'}, use_global_device_ids=true, to_apply=%region_10.11 | all-reduce | flops 2 | bytes 16 | tf_op jit(solution)/shard_map/psum | solution.py:16
  (14 shorter events, 0.2 us)
Async XLA Ops:
  44.3 48.0 %copy-start.3 = (u32[32]{0:T(128)S(1)}, u32[32]{0:T(128)}, u32[]{:S(2)}) copy-start(u32[32]{0:T(128)} %constant.69) | copy-start | bytes 388
  44.3 50.2 %copy-start.2 = (s32[1,3]{1,0:T(1,128)S(1)}, s32[1,3]{1,0:T(1,128)}, u32[]{:S(2)}) copy-start(s32[1,3]{1,0:T(1,128)} %param.13) | copy-start | bytes 40
  92.2 32.6 %copy-start = (f32[1,3]{1,0:T(1,128)S(1)}, f32[1,3]{1,0:T(1,128)}, u32[]{:S(2)}) copy-start(f32[1,3]{1,0:T(1,128)} %param.14) | copy-start | bytes 40
  92.2 32.6 %copy-start.1 = (f32[1,3]{1,0:T(1,128)S(1)}, f32[1,3]{1,0:T(1,128)}, u32[]{:S(2)}) copy-start(f32[1,3]{1,0:T(1,128)} %param.15) | copy-start | bytes 40
